TPU v7x, 16 devices: a whole 2x2x2 slice. The times are simulated.
16 devices in a mesh: rep: 1, dp: 16 (over x, y, z, core).
Axes of the slice: x: 2, y: 2, z: 2, core: 2. Of those that a mesh axis runs over, the one named last changes fastest.
Arguments:
- x: bfloat16 [16, 2048, 1024], P(('rep', 'dp'))
- dy: bfloat16 [16, 2048, 1024], P(('rep', 'dp'))
- w_gate: bfloat16 [2, 1024, 2560], P(None, 'dp')
- w_up: bfloat16 [2, 1024, 2560], P(None, 'dp')
- w_down: bfloat16 [2, 2560, 1024], P(None, 'dp')
Outputs:
- output 1: bfloat16 [16, 2048, 1024], P(('rep', 'dp'))
- output 2: bfloat16 [2, 1024, 2560], P('rep', 'dp')
- output 3: bfloat16 [2, 1024, 2560], P('rep', 'dp')
- output 4: bfloat16 [2, 2560, 1024], P('rep', 'dp')
All inputs are finite; a program needn't handle non-finite values.
Results may differ from a plain program's by a relative error of at most 0.018.
Values are sent between devices in bfloat16 or wider.
A program may use at most 2 GiB of HBM per device.

v0:
```python
import functools

import jax
import jax.numpy as jnp
from jax import lax
from jax.experimental import pallas as pl
from jax.experimental.pallas import tpu as pltpu
from jax.sharding import PartitionSpec as P

F32, BF16 = jnp.float32, jnp.bfloat16
S = jax.ShapeDtypeStruct
MESH = pl.DeviceIdType.MESH
ANY = pl.BlockSpec(memory_space=pl.ANY)
DMA = pltpu.SemaphoreType.DMA
CUBE = (4, 2, 1)
LIMIT = 67_043_328


def dot(a, b, ca, cb):
    return lax.dot_general(a, b, (((ca,), (cb,)), ((), ())), preferred_element_type=F32)


def whole(*shape):
    return pl.BlockSpec(shape, lambda i: (0,) * len(shape), pipeline_mode=pl.Buffered(1))


def rows(mt, cols):
    return pl.BlockSpec((mt, cols), lambda i: (i, 0))


def columns(n, nt):
    return pl.BlockSpec((n, nt), lambda i: (0, i))


class Here:
    def __init__(self):
        me, rep = lax.axis_index("dp"), lax.axis_index("rep")
        chip, self.core = me // 2, me % 2
        self.at = at = [(chip // d) % 2 for d in CUBE]
        own = [c * d for c, d in zip(at, CUBE)]
        far = [d - o for o, d in zip(own, CUBE)]
        self.other = 1 - self.core
        pick = lambda r: [f if r & d else o for o, f, d in zip(own, far, CUBE)]
        self.chips = [sum(pick(r)[1:], pick(r)[0]) for r in range(8)]
        self.devices = {d: (rep, self.chips[d] * 2 + self.core) for d in CUBE}
        self.devices[0] = (rep, chip * 2 + self.other)

    def meet(self):
        barrier = pltpu.get_barrier_semaphore()
        for d in (*CUBE, 0):
            pl.semaphore_signal(barrier, 1, device_id=self.devices[d], device_id_type=MESH)
        pl.semaphore_wait(barrier, 4)

    def remote(self, src, dst, send, recv, d):
        return pltpu.make_async_remote_copy(
            src_ref=src, dst_ref=dst, send_sem=send, recv_sem=recv, device_id=self.devices[d], device_id_type=MESH
        )


def stripes(cols, first):
    tiles = cols // 128
    cut = [tiles // 3 + (1 if (p + first) % 3 < tiles % 3 else 0) for p in range(3)]
    out, at = [], 0
    for p in range(3):
        out.append((slice(at * 128, (at + cut[p]) * 128), CUBE[p:] + CUBE[:p]))
        at += cut[p]
    return out


class Gather:
    def __init__(self, here, mats, sems):
        self.here = here
        self.mats, (self.send, self.recv, self.dsend, self.drecv, self.local) = mats, sems

    @staticmethod
    def scratch(n):
        return [DMA((n, 3, 7)), DMA((n, 3, 7)), DMA((n, 3, 8)), DMA((n, 3, 8)), DMA((n,))]

    def each(self):
        for m, (src, dst) in enumerate(self.mats):
            for p, (cols, order) in enumerate(stripes(src.shape[-1], m)):
                yield m, p, src, dst, cols, order

    def block(self, item, r, other=False):
        m, p, src, dst, cols, order = item
        here = self.here
        return dst.at[here.chips[r], here.other if other else here.core, :, cols]

    def hop(self, item, j, d):
        m, p, src, dst, cols, order = item
        here = src.at[0, :, cols] if j == 0 else self.block(item, j)
        return self.here.remote(here, self.block(item, j), self.send.at[m, p, (j ^ d) - 1], self.recv.at[m, p, (j ^ d) - 1], d)

    def arrived(self, item, r):
        m, p = item[:2]
        self.here.remote(self.block(item, r), self.block(item, r), self.send.at[m, p, r - 1], self.recv.at[m, p, r - 1], 1).wait_recv()

    def hand(self, item, r):
        m, p, src, dst, cols, order = item
        here = src.at[0, :, cols] if r == 0 else self.block(item, r)
        return self.here.remote(here, self.block(item, r), self.dsend.at[m, p, r], self.drecv.at[m, p, r], 0)

    def stage(self, s):
        items = list(self.each())
        if s == 0:
            for n in range(3):
                for it in items:
                    self.hop(it, 0, it[5][n]).start()
            for it in items:
                self.hand(it, 0).start()
            for m, (src, dst) in enumerate(self.mats):
                pltpu.make_async_copy(src.at[0], dst.at[self.here.chips[0], self.here.core], self.local.at[m]).start()
        if s == 1:
            for it in items:
                d0, d1, d2 = it[5]
                self.arrived(it, d0)
                self.hop(it, d0, d1).start()
                self.hop(it, d0, d2).start()
                self.hand(it, d0).start()
        if s == 2:
            for it in items:
                d0, d1, d2 = it[5]
                for r in (d1, d0 ^ d1):
                    self.arrived(it, r)
                    self.hop(it, r, d2).start()
                    self.hand(it, r).start()
        if s == 3:
            for it in items:
                d0, d1, d2 = it[5]
                for r in (d2, d0 ^ d2, d1 ^ d2, 7):
                    self.arrived(it, r)
                    self.hand(it, r).start()
        if s == 4:
            for it in items:
                m, p = it[:2]
                d0, d1, d2 = it[5]
                for r in range(8):
                    self.here.remote(
                        self.block(it, r, True), self.block(it, r, True), self.dsend.at[m, p, r], self.drecv.at[m, p, r], 0
                    ).wait_recv()
                    self.hand(it, r).wait_send()
                for j, d in ((0, d0), (0, d1), (d0, d1), (0, d2), (d0, d2), (d1, d2), (d0 ^ d1, d2)):
                    self.hop(it, j, d).wait_send()
            for m, (src, dst) in enumerate(self.mats):
                pltpu.make_async_copy(src.at[0], dst.at[self.here.chips[0], self.here.core], self.local.at[m]).wait()


class Scatter:
    def __init__(self, here, mats, bufs):
        self.here, self.mats, self.bufs = here, mats, bufs

    @staticmethod
    def scratch(shapes):
        out = []
        for r, c in shapes:
            out += [pltpu.VMEM((n, r, c), BF16) for n in (8, 4, 2, 1)]
            out += [pltpu.VMEM((n, r, c), BF16) for n in (4, 2, 1)]
            out += [DMA((3, 8)), DMA((3, 8)), DMA((3, 7)), DMA((3, 7))]
        return out

    PER = 11

    def each(self):
        for m, (keep, give, out) in enumerate(self.mats):
            b = self.bufs[m * self.PER : (m + 1) * self.PER]
            for p, (cols, order) in enumerate(stripes(keep.shape[-1], m)):
                yield p, keep, give, out, b[:4], b[4:7], b[7:], cols, order

    @staticmethod
    def groups(order):
        d0, d1, d2 = order
        return [[d1, d1 ^ d2, d2, 0], [d2, 0], [0]]

    def hand(self, it, r):
        p, keep, give, out, inn, leave, sems, cols, order = it
        return self.here.remote(give(r).at[:, cols], inn[0].at[r, :, cols], sems[0].at[p, r], sems[1].at[p, r], 0)

    def hop(self, it, s, n):
        p, keep, give, out, inn, leave, sems, cols, order = it
        k = (0, 4, 6)[s] + n
        return self.here.remote(leave[s].at[n, :, cols], inn[s + 1].at[n, :, cols], sems[2].at[p, k], sems[3].at[p, k], order[s])

    def total(self, it, r, upto):
        p, keep, give, out, inn, leave, sems, cols, order = it
        t = keep[r, :, cols].astype(F32) + inn[0][r, :, cols].astype(F32)
        for s in range(upto):
            t = t + inn[s + 1][self.groups(order)[s].index(r), :, cols].astype(F32)
        return t

    def stage(self, s):
        items = list(self.each())
        if s == 0:
            for first in (True, False):
                for it in items:
                    for r in range(8):
                        if bool(r & it[8][0]) == first:
                            self.hand(it, r).start()
            return
        for it in items:
            out, leave, cols, order = it[3], it[5], it[7], it[8]
            groups, h = self.groups(order), s - 1
            going = [r ^ order[h] for r in groups[h]] if s < 4 else [0]
            for n, r in enumerate(going):
                self.hand(it, r).wait_recv()
                for k in range(h):
                    self.hop(it, k, groups[k].index(r)).wait_recv()
                t = self.total(it, r, h).astype(BF16)
                if s < 4:
                    leave[h][n, :, cols] = t
                    self.hop(it, h, n).start()
                else:
                    out[:, cols] = t
        if s == 4:
            for it in items:
                for r in range(8):
                    self.hand(it, r).wait_send()
                for h, n in ((0, 4), (1, 2), (2, 1)):
                    for k in range(n):
                        self.hop(it, h, k).wait_send()


def at_steps(here, job, steps, meet=True):
    i = pl.program_id(0)
    for step in sorted(set(steps) - {-1}):

        @pl.when(i == step)
        def _(step=step):
            for s, when in enumerate(steps):
                if when == step:
                    if s == 0 and meet:
                        here.meet()
                    job.stage(s)


def call(body, name, grid, ins, outs, shapes, scratch, args, flops, cid=None):
    params = dict(dimension_semantics=("arbitrary",), vmem_limit_bytes=LIMIT)
    if cid is not None:
        params.update(collective_id=cid, has_side_effects=True)
    kw = dict(
        name=name,
        grid=(grid,),
        in_specs=ins,
        out_specs=outs,
        out_shape=shapes,
        scratch_shapes=scratch,
        compiler_params=pltpu.CompilerParams(**params),
        cost_estimate=pl.CostEstimate(flops=flops, bytes_accessed=flops // 500, transcendentals=0),
    )
    return pl.pallas_call(body, **kw)(*args)


def with_job(compute, kind, n_in, n_out, n_scr, mats, steps_of, grid):
    def body(*refs):
        k = mats * (1 if kind is Gather else 2) if kind else 0
        ins, refs = refs[:n_in], refs[n_in:]
        jin, refs = refs[:k], refs[k:]
        outs, refs = refs[:n_out], refs[n_out:]
        jout, refs = refs[:mats], refs[mats:]
        scr, bufs = refs[:n_scr], refs[n_scr:]
        here = Here() if kind else None
        if kind is Gather:
            job = Gather(here, list(zip(jin, jout)), bufs)
        elif kind is Scatter:
            job = Scatter(here, [(k, lambda r, g=g: g.at[r], o) for k, g, o in zip(jin[::2], jin[1::2], jout)], bufs)
        last = grid - 1
        if kind:
            at_steps(here, job, [s if not s % 1 and (s < last or not n) else -1 for n, s in enumerate(steps_of)])
        if compute and any(s % 1 for s in steps_of or ()):
            compute(*ins, *outs, *scr, lambda: at_steps(here, job, [int(s) if s % 1 else -1 for s in steps_of]))
        elif compute:
            compute(*ins, *outs, *scr)
        if kind:
            at_steps(here, job, [s if not s % 1 and s >= last and n else -1 for n, s in enumerate(steps_of)])

    return body


def fused(name, grid, compute, ins, outs, shapes, scratch, args, flops, cid=None, gather=None, scatter=None, steps=None):
    ins, outs, shapes, scratch, args = list(ins), list(outs), list(shapes), list(scratch), list(args)
    n_in, n_out, n_scr, kind, mats = len(ins), len(outs), len(scratch), None, 0
    if gather:
        kind, mats = Gather, len(gather)
        for w, layer in gather:
            r, c = w.shape[1:]
            ins.append(pl.BlockSpec((1, r, c), lambda i, layer=layer: (layer, 0, 0), pipeline_mode=pl.Buffered(1)))
            args.append(w)
            outs.append(ANY)
            shapes.append(S((8, 2, r, c), BF16))
        scratch += Gather.scratch(mats)
    if scatter:
        kind, mats = Scatter, len(scatter)
        for keep, give in scatter:
            ins += [whole(*keep.shape), ANY]
            args += [keep, give]
            outs.append(whole(*keep.shape[1:]))
            shapes.append(S(keep.shape[1:], BF16))
        scratch += Scatter.scratch([k.shape[1:] for k, _ in scatter])
    body = with_job(compute, kind, n_in, n_out, n_scr, mats, steps, grid)
    return call(body, name, grid, ins, outs, shapes, scratch, args, flops, cid)


def scale_of(wide):
    return lax.rsqrt(jnp.mean(wide * wide, -1, keepdims=True) + 1e-6)


def norm_into(h, a):
    for r in range(0, h.shape[0], 256):
        wide = h[r : r + 256, :].astype(F32)
        a[r : r + 256, :] = (wide * scale_of(wide)).astype(BF16)


def forward(x, w_gate, w_up, w_down):
    (t, d), ff = x.shape, w_gate.shape[2]
    nt, mt = 512, 512
    n, m = ff // nt, t // mt
    kinds = [w_gate, w_up, w_down] * 2

    def body(x, *refs):
        shards, (mg, mu, hid, h1, a1, a0), full = refs[:6], refs[6:12], refs[12:18]
        a, hidden, tiles, wd, asem, tsem, wsem, *sems = refs[18:]
        here, i = Here(), pl.program_id(0)
        jobs = []
        for k, which in enumerate(((0, 1), (2,), (3, 4), (5,))):
            jobs.append(Gather(here, [(shards[q], full[q]) for q in which], sems[5 * k : 5 * k + 5]))
        first, second, third, fourth = (job.stage for job in jobs)
        keep = pltpu.make_async_copy(a, a0, asem)
        take = pltpu.make_async_copy(full[2], wd, wsem)

        def tile(k, act):
            at = pl.ds(pl.multiple_of(k * nt, nt), nt)
            for q in range(2):
                getattr(pltpu.make_async_copy(full[q].at[:, :, :, at], tiles.at[k % 2, q], tsem.at[k % 2, q]), act)()

        @pl.when(i == 0)
        def _():
            here.meet()
            first(0)
            norm_into(x, a)
            keep.start()
            first(1)
            first(2)
            second(0)
            first(3)
            first(4)
            tile(i, "start")

        @pl.when(i == 1)
        def _():
            second(1)

        @pl.when(i == 2)
        def _():
            second(2)
            third(0)

        @pl.when(i == 3)
        def _():
            second(3)

        @pl.when(i == 4)
        def _():
            second(4)
            take.start()
            third(1)

        @pl.when(i == n + 1)
        def _():
            take.wait()
            third(2)
            fourth(0)

        @pl.when((i >= 1) & (i <= n))
        def _():
            k = i - 1
            tile(k, "wait")

            @pl.when(k < n - 1)
            def _():
                tile(k + 1, "start")

            wg, wu = (lambda q=q: tiles[k % 2, q].reshape(d, nt) for q in range(2))

            @pl.loop(0, m)
            def _(q):
                at = pl.ds(pl.multiple_of(q * mt, mt), mt)
                act, mg[at, :], mu[at, :] = activation(dot(a[at, :], wg(), 1, 0), dot(a[at, :], wu(), 1, 0))
                act = act.astype(BF16)
                hid[at, :] = act
                hidden[at, pl.ds(pl.multiple_of(k * nt, nt), nt)] = act

        @pl.when(i > n)
        def _():
            at = pl.ds(pl.multiple_of((i - n - 1) * mt, mt), mt)
            out = dot(hidden[at, :], wd[...].reshape(ff, d), 1, 0).astype(BF16).astype(F32)
            after = (x[at, :].astype(F32) + out).astype(BF16)
            h1[...] = after
            norm_into(after, a1)

        @pl.when(i == n + m)
        def _():
            keep.wait()
            third(3)
            fourth(1)
            fourth(2)
            third(4)
            fourth(3)
            fourth(4)

    late = lambda i: jnp.maximum(i - n - 1, 0)
    tile = pl.BlockSpec((t, nt), lambda i: (0, jnp.clip(i - 1, 0, n - 1)))
    row = pl.BlockSpec((mt, d), lambda i: (late(i), 0))
    ins = [whole(t, d)]
    for k, w in enumerate(kinds):
        ins.append(pl.BlockSpec((1,) + w.shape[1:], lambda i, k=k: (k // 3, 0, 0), pipeline_mode=pl.Buffered(1)))
    gathered = [S((8, 2) + w.shape[1:], BF16) for w in kinds]
    out = call(
        body, "forward", 1 + n + m, ins, [tile, tile, tile, row, row, ANY] + [ANY] * 6,
        [S((t, ff), F32)] * 2 + [S((t, ff), BF16)] + [S((t, d), BF16)] * 3 + gathered,
        [pltpu.VMEM((t, d), BF16), pltpu.VMEM((t, ff), BF16), pltpu.VMEM((2, 2, 8, 2, d // 16, nt), BF16),
         pltpu.VMEM((8, 2, ff // 16, d), BF16), DMA, DMA((2, 2)), DMA]
        + Gather.scratch(2) + Gather.scratch(1) + Gather.scratch(2) + Gather.scratch(1),
        [x, *kinds], 6 * t * d * ff, 0,
    )
    return *out[:6], *(w.reshape(-1, w.shape[-1]) for w in out[6:])


def activation(g, u):
    s = 0.5 * jnp.tanh(0.5 * g) + 0.5
    silu = g * s
    return silu * u, u * (s + silu * (1 - s)), silu


def last_layer(a, wg, wu, wd, g, name, **job):
    t, d = a.shape
    ff, nt, mt = wd.shape[0], 512, 512

    def compute(a, wg, wu, wd, y, bgu, by_wd, hidden):
        @pl.loop(0, t // mt)
        def _(q):
            at = pl.ds(pl.multiple_of(q * mt, mt), mt)
            hid, mg, mu = activation(dot(a[at, :], wg[...], 1, 0), dot(a[at, :], wu[...], 1, 0))
            hidden[at, :] = hid.astype(BF16)
            b = dot(y[at, :], wd[...], 1, 1).astype(BF16).astype(F32)
            bgu[0, at, :] = (b * mg).astype(BF16)
            bgu[1, at, :] = (b * mu).astype(BF16)
        by_wd[...] = dot(hidden[...], y[...], 0, 0).astype(BF16)

    return fused(
        name, ff // nt, compute, [whole(t, d), columns(d, nt), columns(d, nt), rows(nt, d), whole(t, d)],
        [pl.BlockSpec((2, t, nt), lambda i: (0, 0, i)), rows(nt, d)], [S((2, t, ff), BF16), S((ff, d), BF16)],
        [pltpu.VMEM((t, nt), BF16)], [a, wg, wu, wd, g], 8 * t * d * ff, **job,
    )


def by_hidden(g, wd, by_g, by_u, hidden, name, **job):
    t, d = g.shape
    ff, nt, mt = wd.shape[0], 512, 512

    def compute(y, wd, mg, mu, hidden, bgu, by_wd, between=None):
        for at in (slice(r0, r0 + mt) for r0 in range(0, t, mt)):
            b = dot(y[at, :], wd[...], 1, 1).astype(BF16).astype(F32)
            bgu[0, at, :] = (b * mg[at, :]).astype(BF16)
            bgu[1, at, :] = (b * mu[at, :]).astype(BF16)
        if between:
            between()
        by_wd[...] = dot(hidden[...], y[...], 0, 0).astype(BF16)

    tile = columns(t, nt)
    return fused(
        name, ff // nt, compute, [whole(t, d), rows(nt, d), tile, tile, tile],
        [pl.BlockSpec((2, t, nt), lambda i: (0, 0, i)), rows(nt, d)], [S((2, t, ff), BF16), S((ff, d), BF16)], [],
        [g, wd, by_g, by_u, hidden], 4 * t * d * ff, **job,
    )


def layer_end(a, bgu, wg, wu, h, g, by_wd, name, cid, plans):
    t, d = h.shape
    ff, nt, mt, r = bgu.shape[2], 512, 256, d // 16
    n = ff // nt
    first, second = 2 * n, t // mt
    last = first + second - 1

    hold = len(plans) == 2

    def body(a, cols, both, wg, wu, h, g, by_wd, out, dwd, dwg, *refs):
        dwu, (kgu, ggu, tmp, keep, ksem, *bufs) = refs[: 1 + hold], refs[1 + hold :]
        i, here, per = pl.program_id(0), Here(), Scatter.PER
        mats = [
            (keep, lambda j: by_wd.at[here.chips[j] * 2 + here.other], dwd),
            (kgu.at[0], lambda j: ggu.at[0, j], dwg),
            (kgu.at[1], lambda j: ggu.at[1, j], dwu[0]),
        ]
        jobs = [Scatter(here, [mats[k]], bufs[k * per : (k + 1) * per]) for k in range(len(plans))]
        own = [pltpu.make_async_copy(by_wd.at[here.chips[j] * 2 + here.core], keep.at[j], ksem.at[j]) for j in range(8)]
        kept = hold and [pltpu.make_async_copy(src.at[1], dst, ksem.at[q]) for q, (src, dst) in enumerate(zip((kgu, ggu), dwu))]

        @pl.when(i == 0)
        def _():
            for copy in own:
                copy.start()
            here.meet()

        @pl.when(i == 1)
        def _():
            for copy in own:
                copy.wait()

        if hold:

            @pl.when(i == first)
            def _():
                for copy in kept:
                    copy.start()

        for job, plan in zip(jobs, plans):
            at_steps(here, job, [s if s <= last else -1 for s in plan], False)

        @pl.when(i < first)
        def _():
            w = dot(a[...], cols[0], 0, 0).astype(BF16)
            for c in range(16):
                tmp[c // 2, c % 2] = w[c * r : (c + 1) * r, :]
            at = pl.ds(pl.multiple_of((i % n) * nt, nt), nt)
            for j in range(8):
                kgu[i // n, j, :, at] = tmp[here.chips[j], here.core]
                ggu[i // n, j, :, at] = tmp[here.chips[j], here.other]

        @pl.when(i >= first)
        def _():
            b = (dot(both[0], wg[...], 1, 1) + dot(both[1], wu[...], 1, 1)).astype(BF16).astype(F32)
            wide = h[...].astype(F32)
            s = scale_of(wide)
            along = jnp.mean(b * wide, -1, keepdims=True)
            back = (s * (b - wide * (s * s * along))).astype(BF16).astype(F32)
            out[...] = (g[...].astype(F32) + back).astype(BF16)

        for s in range(5):
            for job, plan in zip(jobs, plans):
                if plan[s] > last:
                    at_steps(here, job, [last if q == s else -1 for q in range(5)], False)
        if hold:

            @pl.when(i == last)
            def _():
                for copy in kept:
                    copy.wait()

    late = lambda i: jnp.maximum(i - first, 0)
    row = pl.BlockSpec((mt, d), lambda i: (late(i), 0))
    early = lambda i: jnp.minimum(i, first - 1)
    shapes = [(by_wd.shape[0] // 16, d), (r, ff), (r, ff)][: len(plans)]
    blocks = by_wd.reshape(16, -1, d)
    return call(
        body, name, first + second,
        [
            whole(t, d),
            pl.BlockSpec((1, t, nt), lambda i: (early(i) // n, 0, early(i) % n)),
            pl.BlockSpec((2, mt, ff), lambda i: (0, late(i), 0)),
            whole(d, ff), whole(d, ff), row, row, ANY,
        ],
        [row] + [whole(*s) for s in shapes] + [ANY, ANY] * hold,
        [S((t, d), BF16)] + [S(s, BF16) for s in shapes] + [S((8, r, ff), BF16)] * (2 * hold),
        [pltpu.VMEM((2, 8, r, ff), BF16), pltpu.VMEM((2, 8, r, ff), BF16), pltpu.VMEM((8, 2, r, nt), BF16),
         pltpu.VMEM((8,) + shapes[0], BF16), DMA((8,))] + Scatter.scratch(shapes),
        [a, bgu, bgu, wg, wu, h, g, blocks], 8 * t * d * ff, cid,
    )


def results(g, lower, upper):
    (t, d), mt = g.shape, 512
    pairs = list(zip(lower, upper))

    def body(g, *refs):
        out, stacks, ins = refs[6], refs[7:], refs[:6]
        out[0] = g[...]

        @pl.when(pl.program_id(0) == 0)
        def _():
            for k, to in enumerate(stacks):
                to[0], to[1] = ins[2 * k][...], ins[2 * k + 1][...]

    return call(
        body, "results", t // mt, [rows(mt, d)] + [whole(*w.shape) for pair in pairs for w in pair],
        [pl.BlockSpec((1, mt, d), lambda i: (0, i, 0))] + [whole(2, *w.shape) for w in lower],
        [S((1, t, d), BF16)] + [S((2, *w.shape), BF16) for w in lower], [], [g, *(w for pair in pairs for w in pair)], 1000,
    )


def solution(mesh):
    def step(x, dy, w_gate, w_up, w_down):
        x, g = x[0], dy[0]
        mg0, mu0, hid0, h1, a1, a0, wg0, wu0, wd0, wg1, wu1, wd1 = forward(x, w_gate, w_up, w_down)
        bgu1, by_wd1 = last_layer(a1, wg1, wu1, wd1, g, "last")
        plan_d, plan_g = [0, 2, 6, 9, 11], [6, 9, 13, 15, 17]
        g, dwd1, dwg1, ku1, gu1 = layer_end(a1, bgu1, wg1, wu1, h1, g, by_wd1, "end1", 3, [plan_d, plan_g])
        bgu0, by_wd0, dwu1 = by_hidden(g, wd0, mg0, mu0, hid0, "dh0", cid=5, scatter=[(ku1, gu1)], steps=[0, 0.5, 2, 3, 4])
        plan_u = [10, 12, 16, 17, 99]
        g, dwd0, dwg0, dwu0 = layer_end(a0, bgu0, wg0, wu0, x, g, by_wd0, "end0", 4, [plan_d, [5, 7, 11, 13, 15], plan_u])
        return results(g, [dwg0, dwu0, dwd0], [dwg1, dwu1, dwd1])

    rows_, cols_, out = P(("rep", "dp")), P(None, "dp"), P("rep", "dp")
    return jax.shard_map(
        step, mesh=mesh, in_specs=(rows_, rows_, cols_, cols_, cols_), out_specs=(rows_, out, out, out), check_vma=False
    )
```

profile of v0, /device:TPU:0, one launch (start us, length us, event | category | flops | bytes accessed | tf_op | source)
XLA Modules:
  0.0 371.5 jit_solution(13986342365371513105)
XLA Ops:
  0.6 121.7 %forward.1 = (f32[2048,2560]{1,0:T(8,128)}, f32[2048,2560]{1,0:T(8,128)}, bf16[2048,2560]{1,0:T(8,128)(2,1)}, bf16[2048,1024]{1,0:T(8,128)(2,1)}, bf16[2048,1024...) custom-call(bf16[2048,1024]{1,0:T(8,128)(2,1)} %bitcast.12, ...), custom_call_target="tpu_custom_call" | custom-call | flops 32212254720 | bytes 64424508 | tf_op jit(solution)/shard_map/forward/pallas_call | solution.py:249
  122.3 54.5 %last.1 = (bf16[2,2048,2560]{2,1,0:T(8,128)(2,1)}, bf16[2560,1024]{1,0:T(8,128)(2,1)}) custom-call(bf16[2048,1024]{1,0:T(8,128)(2,1)} %get-tuple-element.31.refs_0_.a, bf16[1024,2560]{1,0:T(8,128)(2,1)} %bitcast.17, bf16[1024,2560]{1,0:T(8,128)(2,1)} %bitcast.19, bf16[2560,1024]{1,0:T(8,128)(2,1)} %bitcast.22, bf16[2048,1024]{1,0:T(8,128)(2,1)} %bitcast.10), custom_call_target="tpu_custom_call" | custom-call | flops 42949672960 | bytes 85899344 | tf_op jit(solution)/shard_map/last/pallas_call | solution.py:249
  176.9 68.3 %end1.1 = (bf16[2048,1024]{1,0:T(8,128)(2,1)}, bf16[160,1024]{1,0:T(8,128)(2,1)}, bf16[64,2560]{1,0:T(8,128)(2,1)}, bf16[8,64,2560]{2,1,0:T(8,128)(2,1)}, bf16[8,64,2560]{2,1,0:T(8,128)(2,1)}) custom-call(bf16[2048,1024]{1,0:T(8,128)(2,1)} %get-tuple-element.31.refs_0_.a, bf16[2,2048,2560]{2,1,0:T(8,128)(2,1)} %get-tuple-element.35.cols.both, ...), custom_call_target="tpu_custom_call" | custom-call | flops 42949672960 | bytes 85899344 | tf_op jit(solution)/shard_map/end1/pallas_call | solution.py:249
  245.2 42.3 %dh0.1 = (bf16[2,2048,2560]{2,1,0:T(8,128)(2,1)}, bf16[2560,1024]{1,0:T(8,128)(2,1)}, bf16[64,2560]{1,0:T(8,128)(2,1)}) custom-call(bf16[2048,1024]{1,0:T(8,128)(2,1)} %get-tuple-element.38.refs_0_.g, bf16[2560,1024]{1,0:T(8,128)(2,1)} %bitcast.16, f32[2048,2560]{1,0:T(8,128)} %get-tuple-element.40.refs_2_, f32[2048,2560]{1,0:T(8,128)} %get-tuple-element.41.refs_3_, ...), custom_call_target="tpu_custom_call" | custom-call | flops 21474836480 | bytes 42949672 | tf_op jit(solution)/shard_map/dh0/pallas_call | solution.py:249
  287.5 78.0 %end0.1 = (bf16[2048,1024]{1,0:T(8,128)(2,1)}, bf16[160,1024]{1,0:T(8,128)(2,1)}, bf16[64,2560]{1,0:T(8,128)(2,1)}, bf16[64,2560]{1,0:T(8,128)(2,1)}) custom-call(bf16[2048,1024]{1,0:T(8,128)(2,1)} %get-tuple-element.30.a, bf16[2,2048,2560]{2,1,0:T(8,128)(2,1)} %get-tuple-element.45.cols.both, bf16[2,2048,2560]{2,1,0:T(8,128)(2,1)} %get-tuple-element.45.cols.both, ...), custom_call_target="tpu_custom_call" | custom-call | flops 42949672960 | bytes 85899344 | tf_op jit(solution)/shard_map/end0/pallas_call | solution.py:249
  365.5 6.1 %results.1 = (bf16[1,2048,1024]{2,1,0:T(8,128)(2,1)}, bf16[2,64,2560]{2,1,0:T(8,128)(2,1)}, bf16[2,64,2560]{2,1,0:T(8,128)(2,1)}, bf16[2,160,1024]{2,1,0:T(8,128)(2,1)}) custom-call(bf16[2048,1024]{1,0:T(8,128)(2,1)} %get-tuple-element.49.g, bf16[64,2560]{1,0:T(8,128)(2,1)} %get-tuple-element.50.refs_0_, bf16[64,2560]{1,0:T(8,128)(2,1)} %get-tuple-element.51.refs_1_, ...), custom_call_target="tpu_custom_call" | custom-call | flops 1000 | bytes 2 | tf_op jit(solution)/shard_map/results/pallas_call | solution.py:249
where the time goes:
time: 372 us
  Pallas kernels  371 us (100%)
    pallas_call x6, Pallas kernels, call(): return pl.pallas_call(body, **kw)(*args)  371 us

commit v1 on v0

--- a/solution.py
+++ b/solution.py
@@ -309,6 +309,18 @@
         a[r : r + 256, :] = (wide * scale_of(wide)).astype(BF16)
 
 
+EVENTS = {
+    0: ((0, 1), (0, 2), (1, 0), (0, 3), (0, 4)),
+    1: ((1, 1), (2, 0)),
+    2: ((1, 2), (3, 0)),
+    4: ((1, 3), (2, 1)),
+    5: ((1, 4),),
+    6: ((2, 2),),
+    7: ((3, 1),),
+    9: ((2, 3), (3, 2), (2, 4), (3, 3), (3, 4)),
+}
+
+
 def forward(x, w_gate, w_up, w_down):
     (t, d), ff = x.shape, w_gate.shape[2]
     nt, mt = 512, 512
@@ -322,7 +334,7 @@
         jobs = []
         for k, which in enumerate(((0, 1), (2,), (3, 4), (5,))):
             jobs.append(Gather(here, [(shards[q], full[q]) for q in which], sems[5 * k : 5 * k + 5]))
-        first, second, third, fourth = (job.stage for job in jobs)
+        first = jobs[0].stage
         keep = pltpu.make_async_copy(a, a0, asem)
         take = pltpu.make_async_copy(full[2], wd, wsem)
 
@@ -331,43 +343,29 @@
             for q in range(2):
                 getattr(pltpu.make_async_copy(full[q].at[:, :, :, at], tiles.at[k % 2, q], tsem.at[k % 2, q]), act)()
 
+        def run(events):
+            for job, stage in events:
+                jobs[job].stage(stage)
+
         @pl.when(i == 0)
         def _():
             here.meet()
             first(0)
             norm_into(x, a)
             keep.start()
-            first(1)
-            first(2)
-            second(0)
-            first(3)
-            first(4)
+            run(EVENTS[0])
             tile(i, "start")
 
-        @pl.when(i == 1)
-        def _():
-            second(1)
-
-        @pl.when(i == 2)
-        def _():
-            second(2)
-            third(0)
-
-        @pl.when(i == 3)
-        def _():
-            second(3)
-
-        @pl.when(i == 4)
-        def _():
-            second(4)
-            take.start()
-            third(1)
-
-        @pl.when(i == n + 1)
-        def _():
-            take.wait()
-            third(2)
-            fourth(0)
+        for k in range(1, n + m):
+            if k in EVENTS or k in (n, n + 1):
+
+                @pl.when(i == k)
+                def _(k=k):
+                    run(EVENTS.get(k, ()))
+                    if k == n:
+                        take.start()
+                    if k == n + 1:
+                        take.wait()
 
         @pl.when((i >= 1) & (i <= n))
         def _():
@@ -399,12 +397,7 @@
         @pl.when(i == n + m)
         def _():
             keep.wait()
-            third(3)
-            fourth(1)
-            fourth(2)
-            third(4)
-            fourth(3)
-            fourth(4)
+            run(EVENTS[n + m])
 
     late = lambda i: jnp.maximum(i - n - 1, 0)
     tile = pl.BlockSpec((t, nt), lambda i: (0, jnp.clip(i - 1, 0, n - 1)))
@@ -432,7 +425,7 @@
 
 def last_layer(a, wg, wu, wd, g, name, **job):
     t, d = a.shape
-    ff, nt, mt = wd.shape[0], 512, 512
+    ff, nt, mt = wd.shape[0], 512, 1024
 
     def compute(a, wg, wu, wd, y, bgu, by_wd, hidden):
         @pl.loop(0, t // mt)
@@ -478,12 +471,13 @@
     ff, nt, mt, r = bgu.shape[2], 512, 256, d // 16
     n = ff // nt
     first, second = 2 * n, t // mt
-    last = first + second - 1
+    last = first + second
 
     hold = len(plans) == 2
 
-    def body(a, cols, both, wg, wu, h, g, by_wd, out, dwd, dwg, *refs):
-        dwu, (kgu, ggu, tmp, keep, ksem, *bufs) = refs[: 1 + hold], refs[1 + hold :]
+    def body(a, cols, both, gate_hbm, up_hbm, h, g, by_wd, out, dwd, dwg, *refs):
+        dwu, (both_cores, before, wg, wu, wsem, keep, ksem, *bufs) = refs[: 1 + hold], refs[1 + hold :]
+        kgu, ggu = both_cores.at[0], both_cores.at[1]
         i, here, per = pl.program_id(0), Here(), Scatter.PER
         mats = [
             (keep, lambda j: by_wd.at[here.chips[j] * 2 + here.other], dwd),
@@ -492,11 +486,15 @@
         ]
         jobs = [Scatter(here, [mats[k]], bufs[k * per : (k + 1) * per]) for k in range(len(plans))]
         own = [pltpu.make_async_copy(by_wd.at[here.chips[j] * 2 + here.core], keep.at[j], ksem.at[j]) for j in range(8)]
+        weights = [pltpu.make_async_copy(src, dst, wsem.at[q]) for q, (src, dst) in enumerate(((gate_hbm, wg), (up_hbm, wu)))]
         kept = hold and [pltpu.make_async_copy(src.at[1], dst, ksem.at[q]) for q, (src, dst) in enumerate(zip((kgu, ggu), dwu))]
 
         @pl.when(i == 0)
         def _():
+            before[...] = jnp.zeros_like(before)
             for copy in own:
+                copy.start()
+            for copy in weights:
                 copy.start()
             here.meet()
 
@@ -518,21 +516,30 @@
         @pl.when(i < first)
         def _():
             w = dot(a[...], cols[0], 0, 0).astype(BF16)
+            at = pl.ds(pl.multiple_of((i % n) * nt, nt), nt)
             for c in range(16):
-                tmp[c // 2, c % 2] = w[c * r : (c + 1) * r, :]
-            at = pl.ds(pl.multiple_of((i % n) * nt, nt), nt)
-            for j in range(8):
-                kgu[i // n, j, :, at] = tmp[here.chips[j], here.core]
-                ggu[i // n, j, :, at] = tmp[here.chips[j], here.other]
-
-        @pl.when(i >= first)
-        def _():
-            b = (dot(both[0], wg[...], 1, 1) + dot(both[1], wu[...], 1, 1)).astype(BF16).astype(F32)
-            wide = h[...].astype(F32)
+                both_cores[here.other if c % 2 else here.core, i // n, here.chips[c // 2], :, at] = w[c * r : (c + 1) * r, :]
+
+        @pl.when(i == first)
+        def _():
+            for copy in weights:
+                copy.wait()
+
+        def back():
+            b, wide = before[...].astype(F32), h[...].astype(F32)
             s = scale_of(wide)
             along = jnp.mean(b * wide, -1, keepdims=True)
-            back = (s * (b - wide * (s * s * along))).astype(BF16).astype(F32)
-            out[...] = (g[...].astype(F32) + back).astype(BF16)
+            way = (s * (b - wide * (s * s * along))).astype(BF16).astype(F32)
+            out[...] = (g[...].astype(F32) + way).astype(BF16)
+
+        @pl.when((i >= first) & (i < last))
+        def _():
+            back()
+            before[...] = (dot(both[0], wg[...], 1, 1) + dot(both[1], wu[...], 1, 1)).astype(BF16)
+
+        @pl.when(i == last)
+        def _():
+            back()
 
         for s in range(5):
             for job, plan in zip(jobs, plans):
@@ -545,22 +552,22 @@
                 for copy in kept:
                     copy.wait()
 
-    late = lambda i: jnp.maximum(i - first, 0)
-    row = pl.BlockSpec((mt, d), lambda i: (late(i), 0))
+    late = lambda i: jnp.clip(i - first, 0, second - 1)
+    row = pl.BlockSpec((mt, d), lambda i: (jnp.maximum(i - first - 1, 0), 0))
     early = lambda i: jnp.minimum(i, first - 1)
     shapes = [(by_wd.shape[0] // 16, d), (r, ff), (r, ff)][: len(plans)]
     blocks = by_wd.reshape(16, -1, d)
     return call(
-        body, name, first + second,
+        body, name, last + 1,
         [
             whole(t, d),
             pl.BlockSpec((1, t, nt), lambda i: (early(i) // n, 0, early(i) % n)),
             pl.BlockSpec((2, mt, ff), lambda i: (0, late(i), 0)),
-            whole(d, ff), whole(d, ff), row, row, ANY,
+            ANY, ANY, row, row, ANY,
         ],
         [row] + [whole(*s) for s in shapes] + [ANY, ANY] * hold,
         [S((t, d), BF16)] + [S(s, BF16) for s in shapes] + [S((8, r, ff), BF16)] * (2 * hold),
-        [pltpu.VMEM((2, 8, r, ff), BF16), pltpu.VMEM((2, 8, r, ff), BF16), pltpu.VMEM((8, 2, r, nt), BF16),
+        [pltpu.VMEM((2, 2, 8, r, ff), BF16), pltpu.VMEM((mt, d), BF16), pltpu.VMEM((d, ff), BF16), pltpu.VMEM((d, ff), BF16), DMA((2,)),
          pltpu.VMEM((8,) + shapes[0], BF16), DMA((8,))] + Scatter.scratch(shapes),
         [a, bgu, bgu, wg, wu, h, g, blocks], 8 * t * d * ff, cid,
     )
@@ -594,8 +601,8 @@
         plan_d, plan_g = [0, 2, 6, 9, 11], [6, 9, 13, 15, 17]
         g, dwd1, dwg1, ku1, gu1 = layer_end(a1, bgu1, wg1, wu1, h1, g, by_wd1, "end1", 3, [plan_d, plan_g])
         bgu0, by_wd0, dwu1 = by_hidden(g, wd0, mg0, mu0, hid0, "dh0", cid=5, scatter=[(ku1, gu1)], steps=[0, 0.5, 2, 3, 4])
-        plan_u = [10, 12, 16, 17, 99]
-        g, dwd0, dwg0, dwu0 = layer_end(a0, bgu0, wg0, wu0, x, g, by_wd0, "end0", 4, [plan_d, [5, 7, 11, 13, 15], plan_u])
+        plan_u = [10, 12, 16, 18, 99]
+        g, dwd0, dwg0, dwu0 = layer_end(a0, bgu0, wg0, wu0, x, g, by_wd0, "end0", 4, [plan_d, [5, 7, 11, 14, 16], plan_u])
         return results(g, [dwg0, dwu0, dwd0], [dwg1, dwu1, dwd1])
 
     rows_, cols_, out = P(("rep", "dp")), P(None, "dp"), P("rep", "dp")

time: 372 us -> 362 us (0.973)
  Pallas kernels: 371 us -> 361 us
    pallas_call x6, Pallas kernels: 371 us -> 361 us  [call(): return pl.pallas_call(body, **kw)(*args)]
where the time goes in v1:
time: 362 us
  Pallas kernels  361 us (100%)
    pallas_call x6, Pallas kernels, call(): return pl.pallas_call(body, **kw)(*args)  361 us

profile of v1, /device:TPU:0, one launch (start us, length us, event | category | flops | bytes accessed | tf_op | source)
XLA Modules:
  0.0 361.9 jit_solution(18161873966771826441)
XLA Ops:
  0.6 121.7 %forward.1 = (f32[2048,2560]{1,0:T(8,128)}, f32[2048,2560]{1,0:T(8,128)}, bf16[2048,2560]{1,0:T(8,128)(2,1)}, bf16[2048,1024]{1,0:T(8,128)(2,1)}, bf16[2048,1024...) custom-call(bf16[2048,1024]{1,0:T(8,128)(2,1)} %bitcast.12, ...), custom_call_target="tpu_custom_call" | custom-call | flops 32212254720 | bytes 64424508 | tf_op jit(solution)/shard_map/forward/pallas_call | solution.py:249
  122.3 53.8 %last.1 = (bf16[2,2048,2560]{2,1,0:T(8,128)(2,1)}, bf16[2560,1024]{1,0:T(8,128)(2,1)}) custom-call(bf16[2048,1024]{1,0:T(8,128)(2,1)} %get-tuple-element.31.refs_0_.a, bf16[1024,2560]{1,0:T(8,128)(2,1)} %bitcast.17, bf16[1024,2560]{1,0:T(8,128)(2,1)} %bitcast.19, bf16[2560,1024]{1,0:T(8,128)(2,1)} %bitcast.22, bf16[2048,1024]{1,0:T(8,128)(2,1)} %bitcast.10), custom_call_target="tpu_custom_call" | custom-call | flops 42949672960 | bytes 85899344 | tf_op jit(solution)/shard_map/last/pallas_call | solution.py:249
  176.1 64.1 %end1.1 = (bf16[2048,1024]{1,0:T(8,128)(2,1)}, bf16[160,1024]{1,0:T(8,128)(2,1)}, bf16[64,2560]{1,0:T(8,128)(2,1)}, bf16[8,64,2560]{2,1,0:T(8,128)(2,1)}, bf16[8,64,2560]{2,1,0:T(8,128)(2,1)}) custom-call(bf16[2048,1024]{1,0:T(8,128)(2,1)} %get-tuple-element.31.refs_0_.a, bf16[2,2048,2560]{2,1,0:T(8,128)(2,1)} %get-tuple-element.35.cols.both, ...), custom_call_target="tpu_custom_call" | custom-call | flops 42949672960 | bytes 85899344 | tf_op jit(solution)/shard_map/end1/pallas_call | solution.py:249
  240.2 42.3 %dh0.1 = (bf16[2,2048,2560]{2,1,0:T(8,128)(2,1)}, bf16[2560,1024]{1,0:T(8,128)(2,1)}, bf16[64,2560]{1,0:T(8,128)(2,1)}) custom-call(bf16[2048,1024]{1,0:T(8,128)(2,1)} %get-tuple-element.38.refs_0_.g, bf16[2560,1024]{1,0:T(8,128)(2,1)} %bitcast.16, f32[2048,2560]{1,0:T(8,128)} %get-tuple-element.40.refs_2_, f32[2048,2560]{1,0:T(8,128)} %get-tuple-element.41.refs_3_, ...), custom_call_target="tpu_custom_call" | custom-call | flops 21474836480 | bytes 42949672 | tf_op jit(solution)/shard_map/dh0/pallas_call | solution.py:249
  282.5 73.3 %end0.1 = (bf16[2048,1024]{1,0:T(8,128)(2,1)}, bf16[160,1024]{1,0:T(8,128)(2,1)}, bf16[64,2560]{1,0:T(8,128)(2,1)}, bf16[64,2560]{1,0:T(8,128)(2,1)}) custom-call(bf16[2048,1024]{1,0:T(8,128)(2,1)} %get-tuple-element.30.a, bf16[2,2048,2560]{2,1,0:T(8,128)(2,1)} %get-tuple-element.45.cols.both, bf16[2,2048,2560]{2,1,0:T(8,128)(2,1)} %get-tuple-element.45.cols.both, ...), custom_call_target="tpu_custom_call" | custom-call | flops 42949672960 | bytes 85899344 | tf_op jit(solution)/shard_map/end0/pallas_call | solution.py:249
  355.8 6.1 %results.1 = (bf16[1,2048,1024]{2,1,0:T(8,128)(2,1)}, bf16[2,64,2560]{2,1,0:T(8,128)(2,1)}, bf16[2,64,2560]{2,1,0:T(8,128)(2,1)}, bf16[2,160,1024]{2,1,0:T(8,128)(2,1)}) custom-call(bf16[2048,1024]{1,0:T(8,128)(2,1)} %get-tuple-element.49.g, bf16[64,2560]{1,0:T(8,128)(2,1)} %get-tuple-element.50.refs_0_, bf16[64,2560]{1,0:T(8,128)(2,1)} %get-tuple-element.51.refs_1_, ...), custom_call_target="tpu_custom_call" | custom-call | flops 1000 | bytes 2 | tf_op jit(solution)/shard_map/results/pallas_call | solution.py:249

commit v2 on v1

--- a/solution.py
+++ b/solution.py
@@ -327,14 +327,15 @@
     n, m = ff // nt, t // mt
     kinds = [w_gate, w_up, w_down] * 2
 
-    def body(x, *refs):
+    def body(x_hbm, *refs):
         shards, (mg, mu, hid, h1, a1, a0), full = refs[:6], refs[6:12], refs[12:18]
-        a, hidden, tiles, wd, asem, tsem, wsem, *sems = refs[18:]
+        x, a, hidden, tiles, wd, xsem, asem, tsem, wsem, *sems = refs[18:]
         here, i = Here(), pl.program_id(0)
         jobs = []
         for k, which in enumerate(((0, 1), (2,), (3, 4), (5,))):
             jobs.append(Gather(here, [(shards[q], full[q]) for q in which], sems[5 * k : 5 * k + 5]))
         first = jobs[0].stage
+        bring = pltpu.make_async_copy(x_hbm, x, xsem)
         keep = pltpu.make_async_copy(a, a0, asem)
         take = pltpu.make_async_copy(full[2], wd, wsem)
 
@@ -349,8 +350,10 @@
 
         @pl.when(i == 0)
         def _():
+            bring.start()
             here.meet()
             first(0)
+            bring.wait()
             norm_into(x, a)
             keep.start()
             run(EVENTS[0])
@@ -402,15 +405,15 @@
     late = lambda i: jnp.maximum(i - n - 1, 0)
     tile = pl.BlockSpec((t, nt), lambda i: (0, jnp.clip(i - 1, 0, n - 1)))
     row = pl.BlockSpec((mt, d), lambda i: (late(i), 0))
-    ins = [whole(t, d)]
+    ins = [ANY]
     for k, w in enumerate(kinds):
         ins.append(pl.BlockSpec((1,) + w.shape[1:], lambda i, k=k: (k // 3, 0, 0), pipeline_mode=pl.Buffered(1)))
     gathered = [S((8, 2) + w.shape[1:], BF16) for w in kinds]
     out = call(
         body, "forward", 1 + n + m, ins, [tile, tile, tile, row, row, ANY] + [ANY] * 6,
         [S((t, ff), F32)] * 2 + [S((t, ff), BF16)] + [S((t, d), BF16)] * 3 + gathered,
-        [pltpu.VMEM((t, d), BF16), pltpu.VMEM((t, ff), BF16), pltpu.VMEM((2, 2, 8, 2, d // 16, nt), BF16),
-         pltpu.VMEM((8, 2, ff // 16, d), BF16), DMA, DMA((2, 2)), DMA]
+        [pltpu.VMEM((t, d), BF16), pltpu.VMEM((t, d), BF16), pltpu.VMEM((t, ff), BF16),
+         pltpu.VMEM((2, 2, 8, 2, d // 16, nt), BF16), pltpu.VMEM((8, 2, ff // 16, d), BF16), DMA, DMA, DMA((2, 2)), DMA]
         + Gather.scratch(2) + Gather.scratch(1) + Gather.scratch(2) + Gather.scratch(1),
         [x, *kinds], 6 * t * d * ff, 0,
     )

time: 362 us -> 361 us (level)
  no operation moved by 1% of the time
where the time goes in v2:
time: 361 us
  Pallas kernels  360 us (100%)
    pallas_call x6, Pallas kernels, call(): return pl.pallas_call(body, **kw)(*args)  360 us

profile of v2, /device:TPU:0, one launch (start us, length us, event | category | flops | bytes accessed | tf_op | source)
XLA Modules:
  0.0 360.7 jit_solution(15419984870089819794)
XLA Ops:
  0.6 120.5 %forward.1 = (f32[2048,2560]{1,0:T(8,128)}, f32[2048,2560]{1,0:T(8,128)}, bf16[2048,2560]{1,0:T(8,128)(2,1)}, bf16[2048,1024]{1,0:T(8,128)(2,1)}, bf16[2048,1024...) custom-call(bf16[2048,1024]{1,0:T(8,128)(2,1)} %bitcast.12, ...), custom_call_target="tpu_custom_call" | custom-call | flops 32212254720 | bytes 64424508 | tf_op jit(solution)/shard_map/forward/pallas_call | solution.py:249
  121.1 53.8 %last.1 = (bf16[2,2048,2560]{2,1,0:T(8,128)(2,1)}, bf16[2560,1024]{1,0:T(8,128)(2,1)}) custom-call(bf16[2048,1024]{1,0:T(8,128)(2,1)} %get-tuple-element.31.refs_0_.a, bf16[1024,2560]{1,0:T(8,128)(2,1)} %bitcast.17, bf16[1024,2560]{1,0:T(8,128)(2,1)} %bitcast.19, bf16[2560,1024]{1,0:T(8,128)(2,1)} %bitcast.22, bf16[2048,1024]{1,0:T(8,128)(2,1)} %bitcast.10), custom_call_target="tpu_custom_call" | custom-call | flops 42949672960 | bytes 85899344 | tf_op jit(solution)/shard_map/last/pallas_call | solution.py:249
  174.9 64.1 %end1.1 = (bf16[2048,1024]{1,0:T(8,128)(2,1)}, bf16[160,1024]{1,0:T(8,128)(2,1)}, bf16[64,2560]{1,0:T(8,128)(2,1)}, bf16[8,64,2560]{2,1,0:T(8,128)(2,1)}, bf16[8,64,2560]{2,1,0:T(8,128)(2,1)}) custom-call(bf16[2048,1024]{1,0:T(8,128)(2,1)} %get-tuple-element.31.refs_0_.a, bf16[2,2048,2560]{2,1,0:T(8,128)(2,1)} %get-tuple-element.35.cols.both, ...), custom_call_target="tpu_custom_call" | custom-call | flops 42949672960 | bytes 85899344 | tf_op jit(solution)/shard_map/end1/pallas_call | solution.py:249
  239.0 42.3 %dh0.1 = (bf16[2,2048,2560]{2,1,0:T(8,128)(2,1)}, bf16[2560,1024]{1,0:T(8,128)(2,1)}, bf16[64,2560]{1,0:T(8,128)(2,1)}) custom-call(bf16[2048,1024]{1,0:T(8,128)(2,1)} %get-tuple-element.38.refs_0_.g, bf16[2560,1024]{1,0:T(8,128)(2,1)} %bitcast.16, f32[2048,2560]{1,0:T(8,128)} %get-tuple-element.40.refs_2_, f32[2048,2560]{1,0:T(8,128)} %get-tuple-element.41.refs_3_, ...), custom_call_target="tpu_custom_call" | custom-call | flops 21474836480 | bytes 42949672 | tf_op jit(solution)/shard_map/dh0/pallas_call | solution.py:249
  281.3 73.3 %end0.1 = (bf16[2048,1024]{1,0:T(8,128)(2,1)}, bf16[160,1024]{1,0:T(8,128)(2,1)}, bf16[64,2560]{1,0:T(8,128)(2,1)}, bf16[64,2560]{1,0:T(8,128)(2,1)}) custom-call(bf16[2048,1024]{1,0:T(8,128)(2,1)} %get-tuple-element.30.a, bf16[2,2048,2560]{2,1,0:T(8,128)(2,1)} %get-tuple-element.45.cols.both, bf16[2,2048,2560]{2,1,0:T(8,128)(2,1)} %get-tuple-element.45.cols.both, ...), custom_call_target="tpu_custom_call" | custom-call | flops 42949672960 | bytes 85899344 | tf_op jit(solution)/shard_map/end0/pallas_call | solution.py:249
  354.6 6.1 %results.1 = (bf16[1,2048,1024]{2,1,0:T(8,128)(2,1)}, bf16[2,64,2560]{2,1,0:T(8,128)(2,1)}, bf16[2,64,2560]{2,1,0:T(8,128)(2,1)}, bf16[2,160,1024]{2,1,0:T(8,128)(2,1)}) custom-call(bf16[2048,1024]{1,0:T(8,128)(2,1)} %get-tuple-element.49.g, bf16[64,2560]{1,0:T(8,128)(2,1)} %get-tuple-element.50.refs_0_, bf16[64,2560]{1,0:T(8,128)(2,1)} %get-tuple-element.51.refs_1_, ...), custom_call_target="tpu_custom_call" | custom-call | flops 1000 | bytes 2 | tf_op jit(solution)/shard_map/results/pallas_call | solution.py:249
